TPU v7x, 32 devices: a whole 2x2x4 slice. The times are simulated.
32 devices in a mesh: files: 8 (over z, y), rep: 4 (over x, core).
Axes of the slice: x: 2, y: 2, z: 4, core: 2. Of those that a mesh axis runs over, the one named last changes fastest.
Arguments:
- tile_id: int32 [131072], P(('files', 'rep')), may hold values from 0 to 127, as said below
- pix_row: int32 [131072], P(('files', 'rep')), may hold values from 0 to 31
- pix_col: int32 [131072], P(('files', 'rep')), may hold values from 0 to 127
- point_value: bfloat16 [131072], P(('files', 'rep')), may hold values from -6 to 6
Outputs:
- tile_sums: float32 [128, 32, 128], P('files', 'rep')
Inputs may be any that keep to these rules, and one draw needn't show every extreme that they name: `tile_id`: of the points of one device, at most 2048 lie in tiles of one file group (tile id modulo 8), and on every device some group holds exactly 2048 of them.
All inputs are finite; a program needn't handle non-finite values.
Results may differ from a plain program's by a relative error of at most 0.0003.
Values sent between devices are 32-bit elements; how exact they have to be, the bound alone decides.
A program may use at most 64 MiB of HBM per device.

v0:
```python
import jax
import jax.numpy as jnp
from jax import lax
from jax.sharding import PartitionSpec as P

CW = 4096
TC = 128
TR = 32
BAND = 128


def rasterize(dest_rows, dest_cols, point_vals, row_count, block_size):
    slot_total = dest_rows.shape[0]
    block_size = min(block_size, slot_total)
    block_count = slot_total // block_size
    row_ids = jnp.arange(row_count, dtype=jnp.int32)
    col_ids = jnp.arange(TC, dtype=jnp.int32)

    def accumulate(block_index, running):
        block_rows = lax.dynamic_slice_in_dim(dest_rows, block_index * block_size, block_size)
        block_cols = lax.dynamic_slice_in_dim(dest_cols, block_index * block_size, block_size)
        block_vals = lax.dynamic_slice_in_dim(point_vals, block_index * block_size, block_size)
        row_onehot = (block_rows[:, None] == row_ids[None, :]).astype(jnp.bfloat16)
        spread = jnp.where(
            block_cols[:, None] == col_ids[None, :],
            block_vals[:, None],
            jnp.zeros((), jnp.bfloat16),
        )
        return running + lax.dot_general(
            row_onehot, spread, (((0,), (0,)), ((), ())), preferred_element_type=jnp.float32
        )

    return lax.fori_loop(0, block_count, accumulate, jnp.zeros((row_count, TC), jnp.float32))


def per_device(tile_id, pix_row, pix_col, point_value):
    file_groups = lax.axis_size("files")
    rep_groups = lax.axis_size("rep")
    tile_count = BAND // TR * (CW // TC)
    owned = tile_count // file_groups
    quarter = TR // rep_groups
    tile_owner = tile_id % file_groups
    tile_local = tile_id // file_groups
    row_group = pix_row // quarter
    row_inner = pix_row % quarter
    target = ((row_group * file_groups + tile_owner) * owned + tile_local) * quarter + row_inner
    by_rep = lax.psum_scatter(
        rasterize(
            target,
            pix_col,
            point_value,
            lax.axis_size("rep") * (file_groups * owned * quarter),
            512,
        ),
        "rep",
        scatter_dimension=0,
        tiled=True,
    )
    result = lax.psum_scatter(by_rep, "files", scatter_dimension=0, tiled=True)
    return result.reshape(owned, quarter, TC)


def solution(mesh):
    in_specs = (P(("files", "rep")), P(("files", "rep")), P(("files", "rep")), P(("files", "rep")))
    out_specs = P("files", "rep", None)
    return jax.shard_map(
        per_device, mesh=mesh, in_specs=in_specs, out_specs=out_specs, check_vma=False
    )
```

profile of v0, /device:TPU:0, one launch (start us, length us, event | category | flops | bytes accessed | tf_op | source)
XLA Modules:
  0.0 157.1 jit_solution(815454469261013862)
XLA Ops:
  6.5 0.8 fusion.18
  7.3 40.8 %while.14 = (s32[]{:T(128)}, f32[4096,128]{1,0:T(8,128)S(1)}, s32[4096]{0:T(1024)S(1)}, s32[4096]{0:T(1024)}, bf16[4096]{0:T(1024)(128)(2,1)}, /*index=5*/s32[]{:T(128)}, s32[]{:T(128)}, s32[]{:T(128)}, s32[]{:T(128)}) while((s32[]{:T(128)}, f32[4096,128]{1,0:T(8,128)S(1)}, s32[4096]{0:T(1024)S(1)}, s32[4096]{0:T(1024)}, ...), condition=%wide.region_1.2_spmd.clone, body=%wide.region_0.1_spmd.clone.sunk | while | flops 540147712 | bytes 4209833 | solution.py:33
  7.3 0.8 dynamic_slice.29
  8.9 3.5 %fusion.30 = f32[4096,128]{1,0:T(8,128)S(1)} fusion(s32[512]{0:T(512)S(1)} %dynamic_slice.27, f32[4096,128]{1,0:T(8,128)S(1)} %get-tuple-element.203, pred[]{:T(512)S(6)} %compare.9, s32[512]{0:T(512)S(1)} %dynamic_slice.28, bf16[512]{0:T(512)(128)(2,1)S(1)} %dynamic_slice.29), kind=kOutput, calls=%fused_computation.4.clone.1 | convolution fusion | flops 540147712 | bytes 4199425 | tf_op jit(solution)/shard_map/while/body/eval_jaxpr/dot_general | solution.py:29
  12.4 0.8 dynamic_slice.29
  14.0 3.5 %fusion.30 = f32[4096,128]{1,0:T(8,128)S(1)} fusion(s32[512]{0:T(512)S(1)} %dynamic_slice.27, f32[4096,128]{1,0:T(8,128)S(1)} %get-tuple-element.203, pred[]{:T(512)S(6)} %compare.9, s32[512]{0:T(512)S(1)} %dynamic_slice.28, bf16[512]{0:T(512)(128)(2,1)S(1)} %dynamic_slice.29), kind=kOutput, calls=%fused_computation.4.clone.1 | convolution fusion | flops 540147712 | bytes 4199425 | tf_op jit(solution)/shard_map/while/body/eval_jaxpr/dot_general | solution.py:29
  17.5 0.8 dynamic_slice.29
  19.1 3.5 %fusion.30 = f32[4096,128]{1,0:T(8,128)S(1)} fusion(s32[512]{0:T(512)S(1)} %dynamic_slice.27, f32[4096,128]{1,0:T(8,128)S(1)} %get-tuple-element.203, pred[]{:T(512)S(6)} %compare.9, s32[512]{0:T(512)S(1)} %dynamic_slice.28, bf16[512]{0:T(512)(128)(2,1)S(1)} %dynamic_slice.29), kind=kOutput, calls=%fused_computation.4.clone.1 | convolution fusion | flops 540147712 | bytes 4199425 | tf_op jit(solution)/shard_map/while/body/eval_jaxpr/dot_general | solution.py:29
  22.6 0.8 dynamic_slice.29
  23.4 0.8 dynamic_slice.28
  24.2 3.5 %fusion.30 = f32[4096,128]{1,0:T(8,128)S(1)} fusion(s32[512]{0:T(512)S(1)} %dynamic_slice.27, f32[4096,128]{1,0:T(8,128)S(1)} %get-tuple-element.203, pred[]{:T(512)S(6)} %compare.9, s32[512]{0:T(512)S(1)} %dynamic_slice.28, bf16[512]{0:T(512)(128)(2,1)S(1)} %dynamic_slice.29), kind=kOutput, calls=%fused_computation.4.clone.1 | convolution fusion | flops 540147712 | bytes 4199425 | tf_op jit(solution)/shard_map/while/body/eval_jaxpr/dot_general | solution.py:29
  27.8 0.8 dynamic_slice.29
  29.3 3.5 %fusion.30 = f32[4096,128]{1,0:T(8,128)S(1)} fusion(s32[512]{0:T(512)S(1)} %dynamic_slice.27, f32[4096,128]{1,0:T(8,128)S(1)} %get-tuple-element.203, pred[]{:T(512)S(6)} %compare.9, s32[512]{0:T(512)S(1)} %dynamic_slice.28, bf16[512]{0:T(512)(128)(2,1)S(1)} %dynamic_slice.29), kind=kOutput, calls=%fused_computation.4.clone.1 | convolution fusion | flops 540147712 | bytes 4199425 | tf_op jit(solution)/shard_map/while/body/eval_jaxpr/dot_general | solution.py:29
  32.9 0.8 dynamic_slice.29
  33.6 0.8 dynamic_slice.28
  34.5 3.5 %fusion.30 = f32[4096,128]{1,0:T(8,128)S(1)} fusion(s32[512]{0:T(512)S(1)} %dynamic_slice.27, f32[4096,128]{1,0:T(8,128)S(1)} %get-tuple-element.203, pred[]{:T(512)S(6)} %compare.9, s32[512]{0:T(512)S(1)} %dynamic_slice.28, bf16[512]{0:T(512)(128)(2,1)S(1)} %dynamic_slice.29), kind=kOutput, calls=%fused_computation.4.clone.1 | convolution fusion | flops 540147712 | bytes 4199425 | tf_op jit(solution)/shard_map/while/body/eval_jaxpr/dot_general | solution.py:29
  38.0 0.8 dynamic_slice.29
  38.7 0.8 dynamic_slice.28
  39.6 3.5 %fusion.30 = f32[4096,128]{1,0:T(8,128)S(1)} fusion(s32[512]{0:T(512)S(1)} %dynamic_slice.27, f32[4096,128]{1,0:T(8,128)S(1)} %get-tuple-element.203, pred[]{:T(512)S(6)} %compare.9, s32[512]{0:T(512)S(1)} %dynamic_slice.28, bf16[512]{0:T(512)(128)(2,1)S(1)} %dynamic_slice.29), kind=kOutput, calls=%fused_computation.4.clone.1 | convolution fusion | flops 540147712 | bytes 4199425 | tf_op jit(solution)/shard_map/while/body/eval_jaxpr/dot_general | solution.py:29
  43.1 0.8 dynamic_slice.29
  44.7 3.5 %fusion.30 = f32[4096,128]{1,0:T(8,128)S(1)} fusion(s32[512]{0:T(512)S(1)} %dynamic_slice.27, f32[4096,128]{1,0:T(8,128)S(1)} %get-tuple-element.203, pred[]{:T(512)S(6)} %compare.9, s32[512]{0:T(512)S(1)} %dynamic_slice.28, bf16[512]{0:T(512)(128)(2,1)S(1)} %dynamic_slice.29), kind=kOutput, calls=%fused_computation.4.clone.1 | convolution fusion | flops 540147712 | bytes 4199425 | tf_op jit(solution)/shard_map/while/body/eval_jaxpr/dot_general | solution.py:29
  48.2 1.3 copy-done
  49.6 34.0 %reduce-scatter.3.cloned.1.call-done = f32[1024,128]{1,0:T(8,128)} async-done(((f32[4096,128]{1,0:T(8,128)}), f32[1024,128]{1,0:T(8,128)}) %reduce-scatter.3.cloned.1.call-update) | async-done | bytes 524304 | tf_op jit(solution)/shard_map/reduce_scatter | solution.py:47
  83.6 66.7 %reduce-scatter.5.cloned.1.call-done = f32[128,128]{1,0:T(8,128)} async-done(((f32[1024,128]{1,0:T(8,128)}), f32[128,128]{1,0:T(8,128)}) %reduce-scatter.5.cloned.1.call-update) | async-done | bytes 65552 | tf_op jit(solution)/shard_map/reduce_scatter | solution.py:59
  (19 shorter events, 4.5 us)
Async XLA Ops:
  6.5 77.0 %reduce-scatter.3.cloned.1.call-start = ((), (), s32[]{:S(2)}) async-start(), calls=%async_computation.2 | async-start | bytes 2621440 | tf_op jit(solution)/shard_map/reduce_scatter | solution.py:47
  48.2 1.3 copy-start
  49.5 100.8 %reduce-scatter.5.cloned.1.call-start = ((), (), s32[]{:S(2)}) async-start(), calls=%async_computation.3 | async-start | bytes 589824 | tf_op jit(solution)/shard_map/reduce_scatter | solution.py:59
Sparse Core Ops, SparseCore 0:
  49.6 33.8 reduce-scatter.2
  86.9 63.3 reduce-scatter.4
where the time goes:
time: 158 us; the launch traced here: 157 us
  waiting for transfers between devices  101 us (64%)
  matrix products  27.8 us (18%)
  local copies, waits for them, and re-layouts  14.1 us (9%)
  between operations  13.4 us (8%)
    reduce_scatter x1, waiting for transfers between devices, per_device(): result = lax.psum_scatter(by_rep, 'files', scatter_dimension=0, tiled=True)  66.7 us
    reduce_scatter x1, waiting for transfers between devices, per_device(): lax.psum_scatter(rasterize(target, pix_col, point_value, lax.axis_size('r...  34 us
    dot_general x8, matrix products, accumulate(): lax.dot_general(row_onehot, spread, (((0,), (0,)), ((), ())), preferred_e...  27.8 us
    dynamic_slice x8, local copies, waits for them, and re-layouts, accumulate(): lax.dynamic_slice_in_dim(point_vals, block_index * block_size, block_size)  6.08 us
    dynamic_slice x8, local copies, waits for them, and re-layouts, accumulate(): lax.dynamic_slice_in_dim(dest_cols, block_index * block_size, block_size)  6.07 us
  transfers between devices with their start and end apart: 2, of which 2 were waited for; matrix products, arithmetic and copies ran while one was open for 0% of the time, Pallas kernels for 0%

commit v1 on v0

v1 whole, which is shorter than its diff:
```python
import functools

import jax
import jax.numpy as jnp
from jax import lax
from jax.experimental import pallas as pl
from jax.experimental.pallas import tpu as pltpu
from jax.sharding import PartitionSpec as P

LANES = 128
WIDE = 256
TR = 32
TILES = 128
MESH = pl.DeviceIdType.MESH


def flipped(index, mask, count):
    out = index
    bit = 1
    while bit < count:
        if mask & bit:
            out = out + (1 - 2 * ((index // bit) % 2)) * bit
        bit *= 2
    return out


def kernel(nf, nr, owned, quarter, tile_ref, row_ref, col_ref, val_ref, out_ref,
           pack, got, acc, parts, gsend, grecv, rsend, rrecv):
    f = lax.axis_index("files")
    r = lax.axis_index("rep")
    half = owned * quarter // 2
    band = nr * half
    blocks = tile_ref.shape[0]

    barrier = pltpu.get_barrier_semaphore()
    for k in range(1, nf):
        pl.semaphore_signal(barrier, inc=1, device_id={"files": flipped(f, k, nf)}, device_id_type=MESH)
    for k in range(1, nr):
        pl.semaphore_signal(barrier, inc=1, device_id={"rep": flipped(r, k, nr)}, device_id_type=MESH)

    tile = tile_ref[...]
    prow = row_ref[...]
    owner = tile % nf
    inner = (tile // nf) * quarter + prow % quarter
    cell = (owner * band + (prow // quarter) * half + inner % half) * WIDE
    cell = cell + (inner // half) * LANES + col_ref[...]
    pack[0:blocks, :] = cell.astype(jnp.float32)
    pack[blocks:, :] = val_ref[...]
    acc[...] = jnp.zeros_like(acc)

    pl.semaphore_wait(barrier, nf + nr - 2)

    sends = []
    for k in range(1, nf):
        copy = pltpu.make_async_remote_copy(
            src_ref=pack, dst_ref=got.at[k], send_sem=gsend.at[k], recv_sem=grecv.at[k],
            device_id={"files": flipped(f, k, nf)}, device_id_type=MESH)
        copy.start()
        sends.append(copy)

    def add_points(cells, values):
        first = f * band
        row = jnp.floor(cells * (1.0 / WIDE))
        col = cells - row * WIDE
        row = row - first.astype(jnp.float32)
        col_t = jnp.transpose(col)
        ids16 = lax.broadcasted_iota(jnp.int32, (16, LANES), 0)
        lane = lax.broadcasted_iota(jnp.int32, (LANES, LANES), 1)
        lane_lo = lane.astype(jnp.float32).astype(jnp.bfloat16)
        lane_hi = (lane + LANES).astype(jnp.float32).astype(jnp.bfloat16)
        one = jnp.ones((), jnp.bfloat16)
        zero = jnp.zeros((), jnp.bfloat16)
        lhs = []
        rhs = []
        for j in range(blocks):
            row16 = jnp.broadcast_to(row[j:j + 1, :], (16, LANES)).astype(jnp.bfloat16)
            val16 = jnp.broadcast_to(values[j:j + 1, :], (16, LANES)).astype(jnp.bfloat16)
            lhs.append(jnp.concatenate([
                jnp.where(row16 == (ids16 + 16 * i).astype(jnp.float32).astype(jnp.bfloat16), val16, zero)
                for i in range(band // 16)], axis=0))
            colb = jnp.broadcast_to(col_t[:, j:j + 1], (LANES, LANES)).astype(jnp.bfloat16)
            rhs.append(jnp.concatenate([
                jnp.where(colb == lane_lo, one, zero),
                jnp.where(colb == lane_hi, one, zero)], axis=1))
        total = jnp.dot(jnp.concatenate(lhs, axis=1), jnp.concatenate(rhs, axis=0),
                        preferred_element_type=jnp.float32)
        for q in range(nr):
            acc[q] += total[q * half:(q + 1) * half, :]

    add_points(pack[0:blocks, :], pack[blocks:, :])

    def step(k, carry):
        pltpu.make_async_remote_copy(
            src_ref=pack, dst_ref=got.at[k], send_sem=gsend.at[k], recv_sem=grecv.at[k],
            device_id={"files": (f + 1) % nf}, device_id_type=MESH).wait_recv()
        add_points(got[k, 0:blocks, :], got[k, blocks:, :])
        return carry

    lax.fori_loop(1, nf, step, 0)

    backs = []
    for k in range(1, nr):
        peer = flipped(r, k, nr)
        copy = pltpu.make_async_remote_copy(
            src_ref=acc.at[peer], dst_ref=parts.at[k], send_sem=rsend.at[k], recv_sem=rrecv.at[k],
            device_id={"rep": peer}, device_id_type=MESH)
        copy.start()
        backs.append(copy)
    total = acc[r]
    for k in range(1, nr):
        backs[k - 1].wait_recv()
        total = total + parts[k]
    out_ref[0:half, :] = total[:, :LANES]
    out_ref[half:, :] = total[:, LANES:]
    for copy in sends + backs:
        copy.wait_send()


def solution(mesh):
    nf = mesh.shape["files"]
    nr = mesh.shape["rep"]
    owned = TILES // nf
    quarter = TR // nr
    half = owned * quarter // 2

    def per_device(tile_id, pix_row, pix_col, point_value):
        blocks = tile_id.shape[0] // LANES
        shape = (blocks, LANES)
        vmem = pl.BlockSpec(memory_space=pltpu.VMEM)
        out = pl.pallas_call(
            functools.partial(kernel, nf, nr, owned, quarter),
            out_shape=jax.ShapeDtypeStruct((owned * quarter, LANES), jnp.float32),
            in_specs=[vmem] * 4,
            out_specs=vmem,
            scratch_shapes=[
                pltpu.VMEM((2 * blocks, LANES), jnp.float32),
                pltpu.VMEM((nf, 2 * blocks, LANES), jnp.float32),
                pltpu.VMEM((nr, half, WIDE), jnp.float32),
                pltpu.VMEM((nr, half, WIDE), jnp.float32),
                pltpu.SemaphoreType.DMA((nf,)),
                pltpu.SemaphoreType.DMA((nf,)),
                pltpu.SemaphoreType.DMA((nr,)),
                pltpu.SemaphoreType.DMA((nr,)),
            ],
            compiler_params=pltpu.CompilerParams(collective_id=0, has_side_effects=True),
        )(tile_id.reshape(shape), pix_row.reshape(shape), pix_col.reshape(shape),
          point_value.astype(jnp.float32).reshape(shape))
        return out.reshape(owned, quarter, LANES)

    both = P(("files", "rep"))
    return jax.shard_map(per_device, mesh=mesh, in_specs=(both,) * 4,
                         out_specs=P("files", "rep", None), check_vma=False)
```

time: 158 us -> 24.1 us (0.15)
  waiting for transfers between devices: 101 us -> 0 us
  matrix products: 27.8 us -> 0 us
  Pallas kernels: 0 us -> 20.9 us
  between operations: 13.4 us -> 0.01 us
  local copies, waits for them, and re-layouts: 14.1 us -> 1.47 us
    reduce_scatter x2 -> x0, waiting for transfers between devices: 101 us -> none  [the longest x1 66.7 us: per_device(): result = lax.psum_scatter(by_rep, 'files', scatter_dimension=0, tiled=True)]
    dot_general x8 -> x0, matrix products: 27.8 us -> none  [accumulate(): lax.dot_general(row_onehot, spread, (((0,), (0,)), ((), ())), preferred_e...]
    pallas_call x0 -> x1, Pallas kernels: none -> 20.9 us  [per_device(): pl.pallas_call(functools.partial(kernel, nf, nr, owned, quarter), out_sha...]
    dynamic_slice x24 -> x0, local copies, waits for them, and re-layouts: 12.7 us -> none  [the longest x8 6.08 us: accumulate(): lax.dynamic_slice_in_dim(point_vals, block_index * block_size, block_size)]
  transfers between devices with their start and end apart: 2 -> 0, of which waited for: 2 -> 0; matrix products, arithmetic and copies ran while one was open for 0% -> 0% of each run, Pallas kernels for 0% -> 0%
where the time goes in v1:
time: 24.1 us; the launch traced here: 23.7 us
  Pallas kernels  20.9 us (87%)
  local copies, waits for them, and re-layouts  1.47 us (6%)
  other arithmetic  1.3 us (5%)
    pallas_call x1, Pallas kernels, per_device(): pl.pallas_call(functools.partial(kernel, nf, nr, owned, quarter), out_sha...  20.9 us
    unnamed x1, local copies, waits for them, and re-layouts  1.47 us
    reshape x1, other arithmetic, per_device(): point_value.astype(jnp.float32).reshape(shape)  1.3 us

profile of v1, /device:TPU:0, one launch (start us, length us, event | category | flops | bytes accessed | tf_op | source)
XLA Modules:
  0.0 23.7 jit_solution(9814229016025724760)
XLA Ops:
  0.0 1.3 %bitcast_convert_fusion.val_ref = f32[32,128]{1,0:T(8,128)} fusion(bf16[4096]{0:T(1024)(128)(2,1)} %param.7), kind=kLoop, calls=%fused_computation | loop fusion | flops 4096 | bytes 24576 | tf_op jit(solution)/shard_map/reshape | solution.py:147
  1.3 20.9 %shard_map.46 = f32[128,128]{1,0:T(8,128)} custom-call(s32[32,128]{1,0:T(8,128)} %bitcast.8, s32[32,128]{1,0:T(8,128)} %bitcast.9, s32[32,128]{1,0:T(8,128)} %bitcast.10, f32[32,128]{1,0:T(8,128)} %bitcast_convert_fusion.val_ref), custom_call_target="tpu_custom_call" | custom-call | tf_op jit(solution)/shard_map/pallas_call | solution.py:130
  22.3 1.5 %copy.6 = f32[16,8,128]{2,1,0:T(8,128)} copy(f32[16,8,128]{2,1,0:T(8,128)} %bitcast.7) | data formatting | bytes 131072

commit v2 on v1

--- a/solution.py
+++ b/solution.py
@@ -11,6 +11,8 @@
 WIDE = 256
 TR = 32
 TILES = 128
+SPLIT = 1
+ORDER = (1, 2, 6, 3, 7, 4, 5)
 MESH = pl.DeviceIdType.MESH
 
 
@@ -25,54 +27,63 @@
 
 
 def kernel(nf, nr, owned, quarter, tile_ref, row_ref, col_ref, val_ref, out_ref,
-           pack, got, acc, parts, gsend, grecv, rsend, rrecv):
+           tile_in, row_in, col_in, val_in, got, acc, parts,
+           isem, gsend, grecv, rsend, rrecv):
     f = lax.axis_index("files")
     r = lax.axis_index("rep")
     half = owned * quarter // 2
     band = nr * half
     blocks = tile_ref.shape[0]
 
+    loads = []
+    for i, (src, dst) in enumerate(((tile_ref, tile_in), (row_ref, row_in), (col_ref, col_in), (val_ref, val_in))):
+        load = pltpu.make_async_copy(src, dst, isem.at[i])
+        load.start()
+        loads.append(load)
     barrier = pltpu.get_barrier_semaphore()
     for k in range(1, nf):
         pl.semaphore_signal(barrier, inc=1, device_id={"files": flipped(f, k, nf)}, device_id_type=MESH)
     for k in range(1, nr):
         pl.semaphore_signal(barrier, inc=1, device_id={"rep": flipped(r, k, nr)}, device_id_type=MESH)
 
-    tile = tile_ref[...]
-    prow = row_ref[...]
+    for load in loads:
+        load.wait()
+    tile = tile_in[...]
+    prow = row_in[...]
     owner = tile % nf
     inner = (tile // nf) * quarter + prow % quarter
     cell = (owner * band + (prow // quarter) * half + inner % half) * WIDE
-    cell = cell + (inner // half) * LANES + col_ref[...]
-    pack[0:blocks, :] = cell.astype(jnp.float32)
-    pack[blocks:, :] = val_ref[...]
-    acc[...] = jnp.zeros_like(acc)
+    cell = cell + (inner // half) * LANES + col_in[...]
+    got[0, 0:blocks, :] = cell.astype(jnp.float32)
+    got[0, blocks:, :] = val_in[...].astype(jnp.float32)
 
     pl.semaphore_wait(barrier, nf + nr - 2)
 
     sends = []
-    for k in range(1, nf):
+    for i, k in enumerate(ORDER if nf == 8 else range(1, nf), 1):
         copy = pltpu.make_async_remote_copy(
-            src_ref=pack, dst_ref=got.at[k], send_sem=gsend.at[k], recv_sem=grecv.at[k],
+            src_ref=got.at[0], dst_ref=got.at[i], send_sem=gsend.at[i], recv_sem=grecv.at[i],
             device_id={"files": flipped(f, k, nf)}, device_id_type=MESH)
         copy.start()
         sends.append(copy)
 
+    ids16 = lax.broadcasted_iota(jnp.int32, (16, LANES), 0)
+    lane = lax.broadcasted_iota(jnp.int32, (LANES, LANES), 1)
+    lane_lo = lane.astype(jnp.float32).astype(jnp.bfloat16)
+    lane_hi = (lane + LANES).astype(jnp.float32).astype(jnp.bfloat16)
+    one = jnp.ones((), jnp.bfloat16)
+    zero = jnp.zeros((), jnp.bfloat16)
+    first = (f * band).astype(jnp.float32)
+
+    span = blocks // SPLIT
+
     def add_points(cells, values):
-        first = f * band
         row = jnp.floor(cells * (1.0 / WIDE))
-        col = cells - row * WIDE
-        row = row - first.astype(jnp.float32)
-        col_t = jnp.transpose(col)
-        ids16 = lax.broadcasted_iota(jnp.int32, (16, LANES), 0)
-        lane = lax.broadcasted_iota(jnp.int32, (LANES, LANES), 1)
-        lane_lo = lane.astype(jnp.float32).astype(jnp.bfloat16)
-        lane_hi = (lane + LANES).astype(jnp.float32).astype(jnp.bfloat16)
-        one = jnp.ones((), jnp.bfloat16)
-        zero = jnp.zeros((), jnp.bfloat16)
+        col_t = jnp.transpose(cells - row * WIDE)
+        row = row - first
         lhs = []
         rhs = []
-        for j in range(blocks):
+        for j in range(span):
             row16 = jnp.broadcast_to(row[j:j + 1, :], (16, LANES)).astype(jnp.bfloat16)
             val16 = jnp.broadcast_to(values[j:j + 1, :], (16, LANES)).astype(jnp.bfloat16)
             lhs.append(jnp.concatenate([
@@ -87,16 +98,23 @@
         for q in range(nr):
             acc[q] += total[q * half:(q + 1) * half, :]
 
-    add_points(pack[0:blocks, :], pack[blocks:, :])
+    acc[...] = jnp.zeros_like(acc)
 
-    def step(k, carry):
-        pltpu.make_async_remote_copy(
-            src_ref=pack, dst_ref=got.at[k], send_sem=gsend.at[k], recv_sem=grecv.at[k],
-            device_id={"files": (f + 1) % nf}, device_id_type=MESH).wait_recv()
-        add_points(got[k, 0:blocks, :], got[k, blocks:, :])
+    def step(t, carry):
+        i = t // SPLIT
+        at = (t % SPLIT) * span
+
+        @pl.when(jnp.logical_and(i > 0, t % SPLIT == 0))
+        def _():
+            pltpu.make_async_remote_copy(
+                src_ref=got.at[0], dst_ref=got.at[i], send_sem=gsend.at[i], recv_sem=grecv.at[i],
+                device_id={"files": (f + 1) % nf}, device_id_type=MESH).wait_recv()
+
+        add_points(got[i, pl.ds(pl.multiple_of(at, 8), span), :],
+                   got[i, pl.ds(pl.multiple_of(blocks + at, 8), span), :])
         return carry
 
-    lax.fori_loop(1, nf, step, 0)
+    lax.fori_loop(0, nf * SPLIT, step, 0)
 
     backs = []
     for k in range(1, nr):
@@ -130,13 +148,17 @@
         out = pl.pallas_call(
             functools.partial(kernel, nf, nr, owned, quarter),
             out_shape=jax.ShapeDtypeStruct((owned * quarter, LANES), jnp.float32),
-            in_specs=[vmem] * 4,
+            in_specs=[pl.BlockSpec(memory_space=pl.ANY)] * 4,
             out_specs=vmem,
             scratch_shapes=[
-                pltpu.VMEM((2 * blocks, LANES), jnp.float32),
+                pltpu.VMEM(shape, jnp.int32),
+                pltpu.VMEM(shape, jnp.int32),
+                pltpu.VMEM(shape, jnp.int32),
+                pltpu.VMEM(shape, point_value.dtype),
                 pltpu.VMEM((nf, 2 * blocks, LANES), jnp.float32),
                 pltpu.VMEM((nr, half, WIDE), jnp.float32),
                 pltpu.VMEM((nr, half, WIDE), jnp.float32),
+                pltpu.SemaphoreType.DMA((4,)),
                 pltpu.SemaphoreType.DMA((nf,)),
                 pltpu.SemaphoreType.DMA((nf,)),
                 pltpu.SemaphoreType.DMA((nr,)),
@@ -144,7 +166,7 @@
             ],
             compiler_params=pltpu.CompilerParams(collective_id=0, has_side_effects=True),
         )(tile_id.reshape(shape), pix_row.reshape(shape), pix_col.reshape(shape),
-          point_value.astype(jnp.float32).reshape(shape))
+          point_value.reshape(shape))
         return out.reshape(owned, quarter, LANES)
 
     both = P(("files", "rep"))

time: 24.1 us -> 21.9 us (0.909)
  other arithmetic: 1.3 us -> 0 us
  Pallas kernels: 20.9 us -> 20.1 us
    reshape x1 -> x0, other arithmetic: 1.3 us -> none  [per_device(): point_value.astype(jnp.float32).reshape(shape)]
    pallas_call x1, Pallas kernels: 20.9 us -> 20.1 us  [per_device(): pl.pallas_call(functools.partial(kernel, nf, nr, owned, quarter), out_sha...]
where the time goes in v2:
time: 21.9 us; the launch traced here: 21.6 us
  Pallas kernels  20.1 us (92%)
  local copies, waits for them, and re-layouts  1.47 us (7%)
    pallas_call x1, Pallas kernels, per_device(): pl.pallas_call(functools.partial(kernel, nf, nr, owned, quarter), out_sha...  20.1 us
    unnamed x1, local copies, waits for them, and re-layouts  1.47 us

profile of v2, /device:TPU:0, one launch (start us, length us, event | category | flops | bytes accessed | tf_op | source)
XLA Modules:
  0.0 21.6 jit_solution(6584079098960422833)
XLA Ops:
  0.0 20.1 %shard_map.46 = f32[128,128]{1,0:T(8,128)} custom-call(s32[32,128]{1,0:T(8,128)} %bitcast.6, s32[32,128]{1,0:T(8,128)} %bitcast.7, s32[32,128]{1,0:T(8,128)} %bitcast.8, bf16[32,128]{1,0:T(8,128)(2,1)} %bitcast.9), custom_call_target="tpu_custom_call" | custom-call | tf_op jit(solution)/shard_map/pallas_call | solution.py:148
  20.1 1.5 %copy.6 = f32[16,8,128]{2,1,0:T(8,128)} copy(f32[16,8,128]{2,1,0:T(8,128)} %bitcast.5) | data formatting | bytes 131072
